TPU v7x, 256 devices: a whole 4x4x8 slice. The times are simulated.
256 devices in a mesh: fsdp: 64 (over z, x, core), tp: 4 (over y).
Axes of the slice: x: 4, y: 4, z: 8, core: 2. Of those that a mesh axis runs over, the one named last changes fastest.
Arguments:
- slopes_in: float32 [256, 128, 4096], P(None, 'fsdp', 'tp'), may hold values from -6 to 6
- moments_in: float32 [256, 128, 4096], P(None, 'fsdp', 'tp'), may hold values from -6 to 6
- weights_in: float32 [256, 128, 4096], P(None, 'fsdp', 'tp'), may hold values from -0.1875 to 0.1875
Outputs:
- new_weights: float32 [256, 128, 4096], P(None, 'fsdp', 'tp')
- new_momentum: float32 [256, 128, 4096], P(None, 'fsdp', 'tp')
All inputs are finite; a program needn't handle non-finite values.
Results may differ from a plain program's by a relative error of at most 0.00021.
Values sent between devices are 32-bit elements; how exact they have to be, the bound alone decides.
A program may use at most 128 MiB of HBM per device.

v0:
```python
import jax
import jax.numpy as jnp
from jax import lax
from jax.sharding import PartitionSpec as P

ITERS = 5


hold_rate = 0.8
learn_rate = 1.0


def body(slopes_in, moments_in, weights_in):
    new_momentum = hold_rate * moments_in + slopes_in
    moved = lax.all_to_all(new_momentum, "fsdp", split_axis=0, concat_axis=1, tiled=True)
    whole = lax.all_to_all(moved, "tp", split_axis=0, concat_axis=2, tiled=True)
    iterate = whole * lax.rsqrt(jnp.sum(whole * whole, axis=(1, 2), keepdims=True) + 1e-06)
    for step in range(ITERS):
        gram = jnp.einsum("mik,mjk->mij", iterate, iterate, precision=lax.Precision.HIGHEST)
        mixed = -4.775 * gram + 2.0315 * jnp.einsum(
            "mij,mjk->mik", gram, gram, precision=lax.Precision.HIGHEST
        )
        iterate = 3.4445 * iterate + jnp.einsum(
            "mij,mjk->mik", mixed, iterate, precision=lax.Precision.HIGHEST
        )
    iterate = lax.all_to_all(iterate, "tp", split_axis=2, concat_axis=0, tiled=True)
    back = lax.all_to_all(iterate, "fsdp", split_axis=1, concat_axis=0, tiled=True)
    new_weights = weights_in - learn_rate * back
    return (new_weights, new_momentum)


def solution(mesh):
    return jax.shard_map(
        body,
        mesh=mesh,
        in_specs=(P(None, "fsdp", "tp"), P(None, "fsdp", "tp"), P(None, "fsdp", "tp")),
        out_specs=(P(None, "fsdp", "tp"), P(None, "fsdp", "tp")),
        check_vma=False,
    )
```

profile of v0, /device:TPU:1, one launch (start us, length us, event | category | flops | bytes accessed | tf_op | source)
XLA Modules:
  0.0 231.7 jit_solution(4300610404686914742)
XLA Ops:
  0.6 3.7 %multiply_add_fusion = f32[256,2,1024]{2,1,0:T(2,128)S(1)} fusion(f32[256,2,1024]{2,1,0:T(2,128)} %param.3, f32[256,2,1024]{2,1,0:T(2,128)} %param.4), kind=kLoop, calls=%fused_computation.12 | loop fusion | flops 1048576 | bytes 6291456 | tf_op jit(solution)/shard_map/add | solution.py:14
  4.3 62.5 %all_to_all.63 = f32[256,2,1024]{2,1,0:T(2,128)S(1)} all-to-all(f32[256,2,1024]{2,1,0:T(2,128)S(1)} %multiply_add_fusion), channel_id=1, replica_groups=mesh['fsdp'=64,'tp'=4] {'fsdp'}, dimensions={0} | all-to-all | bytes 4194304 | tf_op jit(solution)/shard_map/all_to_all | solution.py:15
  67.6 2.4 %all_to_all.49 = f32[4,128,1024]{2,1,0:T(8,128)} reshape(f32[4,64,2,1024]{3,2,1,0:T(2,128)S(1)} %bitcast.62) | data formatting | bytes 4194304 | tf_op jit(solution)/shard_map/all_to_all | solution.py:15
  70.0 28.2 %all_to_all.64 = f32[4,128,1024]{2,1,0:T(8,128)S(1)} all-to-all(f32[4,128,1024]{2,1,0:T(8,128)} %all_to_all.49), channel_id=1, replica_groups=mesh['fsdp'=64,'tp'=4] {'tp'}, dimensions={0} | all-to-all | bytes 4194304 | tf_op jit(solution)/shard_map/all_to_all | solution.py:16
  100.1 1.8 fusion.4
  102.1 2.6 %multiply_bitcast_fusion.1 = (f32[1,128,4,1024]{3,1,2,0:T(8,128)}, f32[1,128,4,1024]{3,1,2,0:T(8,128)}) fusion(f32[4,128,1024]{2,1,0:T(8,128)S(1)} %all_to_all.64, f32[]{:T(128)S(6)} %rsqrt.4), kind=kLoop, calls=%fused_computation.14 | loop fusion | flops 1048576 | bytes 6291460 | tf_op jit(solution)/shard_map/mul | solution.py:17
  104.7 1.9 copy.26
  106.6 2.9 %copy.25 = f32[1,128,4,1024]{1,3,2,0:T(8,128)} copy(f32[1,128,4,1024]{3,1,2,0:T(8,128)} %get-tuple-element.3) | data formatting | bytes 4194304 | tf_op jit(solution)/shard_map/mul | solution.py:23
  109.5 3.0 %copy.27 = f32[128,4096]{1,0:T(8,128)} copy(f32[128,4096]{0,1:T(8,128)} %bitcast.63) | data formatting | bytes 4194304 | tf_op jit(solution)/shard_map/mul | solution.py:23
  112.4 3.6 %convolution_add_fusion.4 = f32[128,4096]{1,0:T(8,128)S(1)} fusion(f32[128,4096]{1,0:T(8,128)} %copy.27, f32[128,128]{1,0:T(8,128)S(1)} %fusion.11, f32[128,4096]{0,1:T(8,128)S(1)} %bitcast.61), kind=kOutput, calls=%fused_computation.5 | convolution fusion | flops 805830656 | bytes 6356992 | tf_op jit(solution)/shard_map/mij,mjk->mik/dot_general | solution.py:23
  116.0 1.8 fusion.13
  118.0 2.0 convolution_add_fusion.3
  120.1 1.8 fusion.14
  122.1 2.0 convolution_add_fusion.2
  124.1 1.8 fusion.15
  126.2 2.3 convolution_add_fusion.1
  128.4 1.8 fusion.16
  130.5 2.0 fusion
  132.5 3.7 %copy.28 = f32[1,128,4096]{1,0,2:T(1,128)} copy(f32[1,128,4096]{2,1,0:T(8,128)S(1)} %fusion) | data formatting | bytes 4194304 | tf_op jit(solution)/shard_map/add | solution.py:23
  136.2 26.8 %all_to_all.65 = f32[1,128,4096]{1,0,2:T(1,128)S(1)} all-to-all(f32[1,128,4096]{1,0,2:T(1,128)} %copy.28), channel_id=1, replica_groups=mesh['fsdp'=64,'tp'=4] {'tp'}, dimensions={2} | all-to-all | bytes 4194304 | tf_op jit(solution)/shard_map/all_to_all | solution.py:26
  163.0 2.0 copy.29
  164.9 62.3 %all_to_all.66 = f32[4,128,1024]{2,0,1:T(4,128)S(1)} all-to-all(f32[4,128,1024]{2,0,1:T(4,128)} %bitcast.65), channel_id=1, replica_groups=mesh['fsdp'=64,'tp'=4] {'fsdp'}, dimensions={1} | all-to-all | bytes 4194304 | tf_op jit(solution)/shard_map/all_to_all | solution.py:27
  227.2 1.9 copy.30
  229.2 2.5 %bitcast_subtract_fusion = f32[256,2,1024]{2,1,0:T(2,128)} fusion(f32[256,2,1024]{2,1,0:T(2,128)S(1)} %copy-done.1, f32[64,4,2,1024]{3,2,1,0:T(2,128)S(1)} %copy.30), kind=kLoop, calls=%fused_computation.8 | loop fusion | flops 524288 | bytes 6291456 | tf_op jit(solution)/shard_map/sub | solution.py:28
  (11 shorter events, 3.0 us)
Async XLA Ops:
  4.3 62.5 %copy-start = (f32[256,2,1024]{2,1,0:T(2,128)}, f32[256,2,1024]{2,1,0:T(2,128)S(1)}, u32[]{:S(2)}) copy-start(f32[256,2,1024]{2,1,0:T(2,128)S(1)} %multiply_add_fusion) | copy-start | bytes 6291460
  227.2 1.9 copy-start.1
where the time goes:
time: 233 us; the launch traced here: 232 us
  blocking collectives  180 us (77%)
  matrix products  22 us (9%)
  local copies, waits for them, and re-layouts  18.6 us (8%)
  other arithmetic  9.89 us (4%)
    all_to_all x1, blocking collectives, body(): lax.all_to_all(new_momentum, 'fsdp', split_axis=0, concat_axis=1, tiled=T...  62.5 us
    all_to_all x1, blocking collectives, body(): lax.all_to_all(iterate, 'fsdp', split_axis=1, concat_axis=0, tiled=True)  62.3 us
    all_to_all x1, blocking collectives, body(): whole = lax.all_to_all(moved, 'tp', split_axis=0, concat_axis=2, tiled=True)  28.2 us
    all_to_all x1, blocking collectives, body(): lax.all_to_all(iterate, 'tp', split_axis=2, concat_axis=0, tiled=True)  26.8 us
    dot_general x5, matrix products, body(): jnp.einsum('mij,mjk->mik', mixed, iterate, precision=lax.Precision.HIGHEST)  12 us
    dot_general x5, matrix products, body(): jnp.einsum('mik,mjk->mij', iterate, iterate, precision=lax.Precision.HIGH...  8.95 us
    mul x2, local copies, waits for them, and re-layouts, body(): 3.4445 * iterate  5.84 us

commit v1 on v0

v1 whole, which is shorter than its diff:
```python
import jax
import jax.numpy as jnp
from jax import lax
from jax.experimental import pallas as pl
from jax.experimental.pallas import tpu as pltpu
from jax.sharding import PartitionSpec as P

HOLD = 0.8
RATE = 1.0
CA, CB, CC = 3.4445, -4.775, 2.0315
LANES = 128
SIDE = 128
MESH = pl.DeviceIdType.MESH


def dot(a, b, contract=0):
    return lax.dot_general(
        a,
        b,
        (((1,), (contract,)), ((), ())),
        precision=lax.Precision.HIGHEST,
        preferred_element_type=jnp.float32,
    )


def eye():
    shape = (SIDE, SIDE)
    rows = lax.broadcasted_iota(jnp.int32, shape, 0)
    return (rows == lax.broadcasted_iota(jnp.int32, shape, 1)).astype(jnp.float32)


def poly(gram, one):
    return CA * one + CB * gram + CC * dot(gram, gram)


def three_steps(gram, one):
    scale = lax.rsqrt(jnp.sum(gram * one) + 1e-06)
    gram = gram * (scale * scale)
    first = poly(gram, one)
    gram = dot(dot(first, gram), first)
    second = poly(gram, one)
    both = dot(second, first)
    gram = dot(dot(second, gram), second)
    return dot(poly(gram, one), both) * scale


def two_steps(gram, one):
    first = poly(gram, one)
    gram = dot(dot(first, gram), first)
    return dot(poly(gram, one), first)


def make_kernel(fs, tp, mats, wide):
    chunks = mats // fs
    span = 2 * wide // LANES
    cols = wide // LANES
    part = fs * span
    others = fs - 1

    def kernel(
        slopes, moments, weights, new_w, new_m,
        s_buf, m_buf, recv, res, back, w_buf, x_buf, x3_buf, grams,
        s_sem, m_sem, w_sem, f_send, f_recv, b_send, b_recv, g_send, g_recv,
    ):
        me = lax.axis_index("fsdp")
        col = lax.axis_index("tp")
        z, x, c = me // 8, (me // 2) % 4, me % 2

        def peer(i):
            far, near = i // 8, i % 8
            up = (far + 1) // 2
            step = (far % 2) * up + (1 - far % 2) * (8 - far // 2)
            return ((z + step) % 8) * 8 + ((x + near // 2) % 4) * 2 + (c + near % 2) % 2

        def chunk(k):
            return pl.ds(pl.multiple_of(k * part, part), part)

        def block(k, j):
            return pl.ds(pl.multiple_of(k * part + j * span, span), span)

        def load(k):
            pltpu.make_async_copy(slopes.at[chunk(k)], s_buf.at[chunk(k)], s_sem.at[k]).start()
            pltpu.make_async_copy(moments.at[chunk(k)], m_buf.at[chunk(k)], m_sem.at[k]).start()

        def send(src, dst, k, i, send_sem, recv_sem):
            j = peer(i)
            pltpu.make_async_remote_copy(
                src_ref=src.at[block(k, j)],
                dst_ref=dst.at[block(k, me)],
                send_sem=send_sem,
                recv_sem=recv_sem.at[k],
                device_id=(j, col),
                device_id_type=MESH,
            ).start()

        def send_all(src, dst, k, send_sem, recv_sem):
            def go(i, carry):
                send(src, dst, k, i, send_sem, recv_sem)
                return carry

            lax.fori_loop(1, fs, go, 0)

        def wait_rows(buf, n, sem):
            rows = pl.ds(0, n * span)
            pltpu.make_async_copy(buf.at[rows], buf.at[rows], sem).wait()

        load(0)
        barrier = pltpu.get_barrier_semaphore()

        def greet(i, carry):
            pl.semaphore_signal(barrier, inc=1, device_id=(peer(i), col), device_id_type=MESH)
            return carry

        lax.fori_loop(1, fs, greet, 0)
        for d in range(1, tp):
            pl.semaphore_signal(barrier, inc=1, device_id=(me, (col + d) % tp), device_id_type=MESH)
        for k in range(1, chunks):
            load(k)
        pltpu.make_async_copy(weights, w_buf, w_sem).start()

        def momentum(k, carry):
            pltpu.make_async_copy(slopes.at[chunk(k)], s_buf.at[chunk(k)], s_sem.at[k]).wait()
            pltpu.make_async_copy(moments.at[chunk(k)], m_buf.at[chunk(k)], m_sem.at[k]).wait()
            new_m[chunk(k), :] = HOLD * m_buf[chunk(k), :] + s_buf[chunk(k), :]
            return carry

        momentum(0, 0)
        pl.semaphore_wait(barrier, others + tp - 1)

        def spread(k, carry):
            send_all(new_m, recv, k, f_send, f_recv)
            recv[block(k, me), :] = new_m[block(k, me), :]
            return carry

        spread(0, 0)

        def rest(k, carry):
            momentum(k, 0)
            return spread(k, 0)

        lax.fori_loop(1, chunks, rest, 0)

        one = eye()

        def share(turn, k, value):
            grams[turn, k, col] = value
            copies = []
            for d in range(1, tp):
                copies.append(
                    pltpu.make_async_remote_copy(
                        src_ref=grams.at[turn, k, col],
                        dst_ref=grams.at[turn, k, col],
                        send_sem=g_send.at[turn, d - 1],
                        recv_sem=g_recv.at[turn, k, d - 1],
                        device_id=(me, (col + d) % tp),
                        device_id_type=MESH,
                    )
                )
            for copy in copies:
                copy.start()
            for copy in copies:
                copy.wait()
            total = grams[turn, k, 0]
            for t in range(1, tp):
                total = total + grams[turn, k, t]
            return total

        def work(k, carry):
            wait_rows(recv, others, f_recv.at[k])
            for t in range(cols):
                for r in range(2):
                    x_buf[fs * r : fs * (r + 1), LANES * t : LANES * (t + 1)] = recv[
                        pl.ds(k * part + 2 * t + r, fs, stride=span), :
                    ]
            gram = share(0, k, dot(x_buf[...], x_buf[...], 1))
            mixed = three_steps(gram, one)
            for t in range(0, wide, 256):
                x3_buf[:, t : t + 256] = dot(mixed, x_buf[:, t : t + 256])
            gram = share(1, k, dot(x3_buf[...], x3_buf[...], 1))
            mixed = two_steps(gram, one)
            for t in range(cols):
                out = dot(mixed, x3_buf[:, LANES * t : LANES * (t + 1)])
                for r in range(2):
                    res[pl.ds(k * part + 2 * t + r, fs, stride=span), :] = out[fs * r : fs * (r + 1)]
            send_all(res, back, k, b_send, b_recv)
            back[block(k, me), :] = res[block(k, me), :]
            return carry

        lax.fori_loop(0, chunks, work, 0)
        pltpu.make_async_copy(weights, w_buf, w_sem).wait()

        def finish(k, carry):
            wait_rows(back, others, b_recv.at[k])
            new_w[chunk(k), :] = w_buf[chunk(k), :] - RATE * back[chunk(k), :]
            return carry

        lax.fori_loop(0, chunks, finish, 0)
        wait_rows(new_m, chunks * others, f_send)
        wait_rows(res, chunks * others, b_send)

    total = chunks * part
    buf = pltpu.VMEM((total, LANES), jnp.float32)
    scratch = [buf] * 6 + [
        pltpu.VMEM((SIDE, wide), jnp.float32),
        pltpu.VMEM((SIDE, wide), jnp.float32),
        pltpu.VMEM((2, chunks, tp, SIDE, SIDE), jnp.float32),
    ]
    dma = pltpu.SemaphoreType.DMA
    scratch += [
        dma((chunks,)), dma((chunks,)), dma,
        dma, dma((chunks,)), dma, dma((chunks,)), dma((2, tp - 1)), dma((2, chunks, tp - 1)),
    ]
    hbm = pl.BlockSpec(memory_space=pltpu.HBM)
    return pl.pallas_call(
        kernel,
        out_shape=[jax.ShapeDtypeStruct((total, LANES), jnp.float32)] * 2,
        in_specs=[hbm] * 3,
        out_specs=[pl.BlockSpec(memory_space=pltpu.VMEM)] * 2,
        scratch_shapes=scratch,
        compiler_params=pltpu.CompilerParams(
            collective_id=0, has_side_effects=True, vmem_limit_bytes=40 << 20
        ),
        name="step",
    )


def flat(a):
    m, r, w = a.shape
    return a.reshape(m, r, w // LANES, LANES).transpose(0, 2, 1, 3).reshape(-1, LANES)


def solution(mesh):
    fs, tp = mesh.shape["fsdp"], mesh.shape["tp"]

    def body(slopes_in, moments_in, weights_in):
        mats, rows, wide = slopes_in.shape

        def unflat(a):
            a = a.reshape(mats, wide // LANES, rows, LANES).transpose(0, 2, 1, 3)
            return a.reshape(mats, rows, wide)

        new_w, new_m = make_kernel(fs, tp, mats, wide)(
            flat(slopes_in), flat(moments_in), flat(weights_in)
        )
        return unflat(new_w), unflat(new_m)

    spec = P(None, "fsdp", "tp")
    return jax.shard_map(
        body, mesh=mesh, in_specs=(spec,) * 3, out_specs=(spec,) * 2, check_vma=False
    )
```

time: 233 us -> 123 us (0.53)
  blocking collectives: 180 us -> 0 us
  Pallas kernels: 0 us -> 114 us
  matrix products: 22 us -> 0 us
  local copies, waits for them, and re-layouts: 18.6 us -> 7.41 us
  other arithmetic: 9.89 us -> 0 us
    all_to_all x4 -> x0, blocking collectives: 180 us -> none  [the longest x1 62.5 us: body(): lax.all_to_all(new_momentum, 'fsdp', split_axis=0, concat_axis=1, tiled=T...]
    pallas_call x0 -> x1, Pallas kernels: none -> 114 us  [body(): make_kernel(fs, tp, mats, wide)]
    dot_general x15 -> x0, matrix products: 22 us -> none  [the longest x5 12 us: body(): jnp.einsum('mij,mjk->mik', mixed, iterate, precision=lax.Precision.HIGHEST)]
    mul x3 -> x0, local copies, waits for them, and re-layouts: 7.74 us -> none  [the longest x2 5.84 us: body(): 3.4445 * iterate]
    unnamed x4 -> x8, local copies, waits for them, and re-layouts: 0.01 us -> 7.41 us
    all_to_all x4 -> x0, local copies, waits for them, and re-layouts: 7.13 us -> none  [the longest x2 3.24 us: body(): lax.all_to_all(new_momentum, 'fsdp', split_axis=0, concat_axis=1, tiled=T...]
    add x1 -> x0, local copies, waits for them, and re-layouts: 3.7 us -> none  [body(): 3.4445 * iterate]
    add x1 -> x0, other arithmetic: 3.66 us -> none  [body(): new_momentum = hold_rate * moments_in + slopes_in]
where the time goes in v1:
time: 123 us
  Pallas kernels  114 us (93%)
  local copies, waits for them, and re-layouts  7.41 us (6%)
    pallas_call x1, Pallas kernels, body(): make_kernel(fs, tp, mats, wide)  114 us
    unnamed x8, local copies, waits for them, and re-layouts  7.41 us

profile of v1, /device:TPU:1, one launch (start us, length us, event | category | flops | bytes accessed | tf_op | source)
XLA Modules:
  0.0 122.5 jit_solution(3773837697832371646)
XLA Ops:
  0.6 0.0 copy-start
  0.6 1.6 %copy-done = f32[256,2,1024]{2,1,0:T(2,128)S(1)} copy-done((f32[256,2,1024]{2,1,0:T(2,128)S(1)}, f32[256,2,1024]{2,1,0:T(2,128)}, u32[]{:S(2)}) %copy-start) | copy-done | bytes 2097176
  2.2 0.0 copy-start.1
  2.2 1.6 %copy-done.1 = f32[256,2,1024]{2,1,0:T(2,128)S(1)} copy-done((f32[256,2,1024]{2,1,0:T(2,128)S(1)}, f32[256,2,1024]{2,1,0:T(2,128)}, u32[]{:S(2)}) %copy-start.1) | copy-done | bytes 2097176
  3.8 0.0 copy-start.2
  3.8 1.6 %copy-done.2 = f32[256,2,1024]{2,1,0:T(2,128)S(1)} copy-done((f32[256,2,1024]{2,1,0:T(2,128)S(1)}, f32[256,2,1024]{2,1,0:T(2,128)}, u32[]{:S(2)}) %copy-start.2) | copy-done | bytes 2097176
  5.4 114.5 %step.1 = (f32[4096,128]{1,0:T(8,128)S(1)}, f32[4096,128]{1,0:T(8,128)S(1)}) custom-call(f32[4096,128]{1,0:T(8,128)S(1)} %bitcast.25, f32[4096,128]{1,0:T(8,128)S(1)} %bitcast.26, f32[4096,128]{1,0:T(8,128)S(1)} %bitcast.27), custom_call_target="tpu_custom_call" | custom-call | tf_op jit(solution)/shard_map/step/pallas_call | solution.py:242
  119.9 1.3 %copy.12 = f32[256,2,1024]{2,1,0:T(2,128)} copy(f32[256,2,1024]{2,1,0:T(2,128)S(1)} %bitcast.29) | data formatting | bytes 4194304
  121.2 1.3 %copy.13 = f32[256,2,1024]{2,1,0:T(2,128)} copy(f32[256,2,1024]{2,1,0:T(2,128)S(1)} %bitcast.28) | data formatting | bytes 4194304
Async XLA Ops:
  0.6 1.6 %copy-start = (f32[256,2,1024]{2,1,0:T(2,128)S(1)}, f32[256,2,1024]{2,1,0:T(2,128)}, u32[]{:S(2)}) copy-start(f32[256,2,1024]{2,1,0:T(2,128)} %param.3) | copy-start | bytes 6291460
  2.2 1.6 %copy-start.1 = (f32[256,2,1024]{2,1,0:T(2,128)S(1)}, f32[256,2,1024]{2,1,0:T(2,128)}, u32[]{:S(2)}) copy-start(f32[256,2,1024]{2,1,0:T(2,128)} %param.4) | copy-start | bytes 6291460
  3.8 1.6 %copy-start.2 = (f32[256,2,1024]{2,1,0:T(2,128)S(1)}, f32[256,2,1024]{2,1,0:T(2,128)}, u32[]{:S(2)}) copy-start(f32[256,2,1024]{2,1,0:T(2,128)} %param.5) | copy-start | bytes 6291460

commit v2 on v1

--- a/solution.py
+++ b/solution.py
@@ -10,6 +10,8 @@
 CA, CB, CC = 3.4445, -4.775, 2.0315
 LANES = 128
 SIDE = 128
+RING = 8
+AROUND = (0, 1, 7, 2, 6, 3, 5, 4)
 MESH = pl.DeviceIdType.MESH
 
 
@@ -60,17 +62,28 @@
     def kernel(
         slopes, moments, weights, new_w, new_m,
         s_buf, m_buf, recv, res, back, w_buf, x_buf, x3_buf, grams,
-        s_sem, m_sem, w_sem, f_send, f_recv, b_send, b_recv, g_send, g_recv,
+        s_sem, m_sem, w_sem, f_send, f_recv, b_send, b_recv, g_send, g_recv, ready,
     ):
         me = lax.axis_index("fsdp")
         col = lax.axis_index("tp")
-        z, x, c = me // 8, (me // 2) % 4, me % 2
-
-        def peer(i):
-            far, near = i // 8, i % 8
-            up = (far + 1) // 2
-            step = (far % 2) * up + (1 - far % 2) * (8 - far // 2)
-            return ((z + step) % 8) * 8 + ((x + near // 2) % 4) * 2 + (c + near % 2) % 2
+        z, x, c = me // RING, (me // 2) % 4, me % 2
+
+        rings = [(z + far) % RING * 8 for far in range(RING)]
+
+        def peers(fars, visit):
+            def at(n, carry):
+                near = (x + n // 2) % 4 * 2 + (c + n % 2) % 2
+                for far in fars:
+                    visit(rings[far] + near)
+                return carry
+
+            if 0 in fars:
+                for far in fars:
+                    if far:
+                        visit(rings[far] + x * 2 + c)
+                lax.fori_loop(1, 8, at, 0)
+            else:
+                lax.fori_loop(0, 8, at, 0)
 
         def chunk(k):
             return pl.ds(pl.multiple_of(k * part, part), part)
@@ -82,23 +95,18 @@
             pltpu.make_async_copy(slopes.at[chunk(k)], s_buf.at[chunk(k)], s_sem.at[k]).start()
             pltpu.make_async_copy(moments.at[chunk(k)], m_buf.at[chunk(k)], m_sem.at[k]).start()
 
-        def send(src, dst, k, i, send_sem, recv_sem):
-            j = peer(i)
-            pltpu.make_async_remote_copy(
-                src_ref=src.at[block(k, j)],
-                dst_ref=dst.at[block(k, me)],
-                send_sem=send_sem,
-                recv_sem=recv_sem.at[k],
-                device_id=(j, col),
-                device_id_type=MESH,
-            ).start()
-
-        def send_all(src, dst, k, send_sem, recv_sem):
-            def go(i, carry):
-                send(src, dst, k, i, send_sem, recv_sem)
-                return carry
-
-            lax.fori_loop(1, fs, go, 0)
+        def send_all(src, dst, k, send_sem, recv_sem, fars=AROUND):
+            def send(j):
+                pltpu.make_async_remote_copy(
+                    src_ref=src.at[block(k, j)],
+                    dst_ref=dst.at[block(k, me)],
+                    send_sem=send_sem,
+                    recv_sem=recv_sem.at[k],
+                    device_id=(j, col),
+                    device_id_type=MESH,
+                ).start()
+
+            peers(fars, send)
 
         def wait_rows(buf, n, sem):
             rows = pl.ds(0, n * span)
@@ -107,11 +115,10 @@
         load(0)
         barrier = pltpu.get_barrier_semaphore()
 
-        def greet(i, carry):
-            pl.semaphore_signal(barrier, inc=1, device_id=(peer(i), col), device_id_type=MESH)
-            return carry
-
-        lax.fori_loop(1, fs, greet, 0)
+        def greet(j):
+            pl.semaphore_signal(barrier, inc=1, device_id=(j, col), device_id_type=MESH)
+
+        peers((1, 7, 0), greet)
         for d in range(1, tp):
             pl.semaphore_signal(barrier, inc=1, device_id=(me, (col + d) % tp), device_id_type=MESH)
         for k in range(1, chunks):
@@ -124,16 +131,28 @@
             new_m[chunk(k), :] = HOLD * m_buf[chunk(k), :] + s_buf[chunk(k), :]
             return carry
 
+        def tell(turn):
+            for far in (1, 7):
+                pl.semaphore_signal(
+                    ready.at[turn], inc=1, device_id=(rings[far] + x * 2 + c, col), device_id_type=MESH
+                )
+
+        pl.semaphore_wait(barrier, 3 * 8 - 1 + tp - 1)
+        tell(0)
         momentum(0, 0)
-        pl.semaphore_wait(barrier, others + tp - 1)
+        send_all(new_m, recv, 0, f_send, f_recv, (1, 7, 0))
+        for turn, fars in enumerate(((2, 6), (3, 5), (4,))):
+            pl.semaphore_wait(ready.at[turn], 2)
+            if turn < 2:
+                tell(turn + 1)
+            send_all(new_m, recv, 0, f_send, f_recv, fars)
+        recv[block(0, me), :] = new_m[block(0, me), :]
 
         def spread(k, carry):
             send_all(new_m, recv, k, f_send, f_recv)
             recv[block(k, me), :] = new_m[block(k, me), :]
             return carry
 
-        spread(0, 0)
-
         def rest(k, carry):
             momentum(k, 0)
             return spread(k, 0)
@@ -142,42 +161,52 @@
 
         one = eye()
 
+        def shares(turn, k):
+            return [
+                pltpu.make_async_remote_copy(
+                    src_ref=grams.at[turn, k, col],
+                    dst_ref=grams.at[turn, k, col],
+                    send_sem=g_send.at[turn, d - 1],
+                    recv_sem=g_recv.at[turn, k, d - 1],
+                    device_id=(me, (col + d) % tp),
+                    device_id_type=MESH,
+                )
+                for d in range(1, tp)
+            ]
+
         def share(turn, k, value):
             grams[turn, k, col] = value
-            copies = []
-            for d in range(1, tp):
-                copies.append(
-                    pltpu.make_async_remote_copy(
-                        src_ref=grams.at[turn, k, col],
-                        dst_ref=grams.at[turn, k, col],
-                        send_sem=g_send.at[turn, d - 1],
-                        recv_sem=g_recv.at[turn, k, d - 1],
-                        device_id=(me, (col + d) % tp),
-                        device_id_type=MESH,
-                    )
-                )
-            for copy in copies:
+            for copy in shares(turn, k):
                 copy.start()
-            for copy in copies:
+
+        def shared(turn, k):
+            for copy in shares(turn, k):
                 copy.wait()
             total = grams[turn, k, 0]
             for t in range(1, tp):
                 total = total + grams[turn, k, t]
             return total
 
-        def work(k, carry):
+        def take(k):
             wait_rows(recv, others, f_recv.at[k])
             for t in range(cols):
                 for r in range(2):
                     x_buf[fs * r : fs * (r + 1), LANES * t : LANES * (t + 1)] = recv[
                         pl.ds(k * part + 2 * t + r, fs, stride=span), :
                     ]
-            gram = share(0, k, dot(x_buf[...], x_buf[...], 1))
-            mixed = three_steps(gram, one)
+            share(0, k, dot(x_buf[...], x_buf[...], 1))
+
+        def work(k, carry):
+            mixed = three_steps(shared(0, k), one)
             for t in range(0, wide, 256):
                 x3_buf[:, t : t + 256] = dot(mixed, x_buf[:, t : t + 256])
-            gram = share(1, k, dot(x3_buf[...], x3_buf[...], 1))
-            mixed = two_steps(gram, one)
+            share(1, k, dot(x3_buf[...], x3_buf[...], 1))
+
+            @pl.when(k + 1 < chunks)
+            def _():
+                take(k + 1)
+
+            mixed = two_steps(shared(1, k), one)
             for t in range(cols):
                 out = dot(mixed, x3_buf[:, LANES * t : LANES * (t + 1)])
                 for r in range(2):
@@ -186,6 +215,7 @@
             back[block(k, me), :] = res[block(k, me), :]
             return carry
 
+        take(0)
         lax.fori_loop(0, chunks, work, 0)
         pltpu.make_async_copy(weights, w_buf, w_sem).wait()
 
@@ -209,6 +239,7 @@
     scratch += [
         dma((chunks,)), dma((chunks,)), dma,
         dma, dma((chunks,)), dma, dma((chunks,)), dma((2, tp - 1)), dma((2, chunks, tp - 1)),
+        pltpu.SemaphoreType.REGULAR((3,)),
     ]
     hbm = pl.BlockSpec(memory_space=pltpu.HBM)
     return pl.pallas_call(
@@ -218,12 +249,34 @@
         out_specs=[pl.BlockSpec(memory_space=pltpu.VMEM)] * 2,
         scratch_shapes=scratch,
         compiler_params=pltpu.CompilerParams(
-            collective_id=0, has_side_effects=True, vmem_limit_bytes=40 << 20
+            collective_id=0, has_side_effects=True, vmem_limit_bytes=48 << 20
         ),
         name="step",
     )
 
 
+def store(new_w, new_m):
+    def kernel(w_in, m_in, w_out, m_out, sem):
+        copies = [
+            pltpu.make_async_copy(w_in, w_out, sem.at[0]),
+            pltpu.make_async_copy(m_in, m_out, sem.at[1]),
+        ]
+        for copy in copies:
+            copy.start()
+        for copy in copies:
+            copy.wait()
+
+    return pl.pallas_call(
+        kernel,
+        out_shape=[jax.ShapeDtypeStruct(new_w.shape, new_w.dtype)] * 2,
+        in_specs=[pl.BlockSpec(memory_space=pltpu.VMEM)] * 2,
+        out_specs=[pl.BlockSpec(memory_space=pltpu.HBM)] * 2,
+        scratch_shapes=[pltpu.SemaphoreType.DMA((2,))],
+        compiler_params=pltpu.CompilerParams(vmem_limit_bytes=8 << 20),
+        name="store",
+    )(new_w, new_m)
+
+
 def flat(a):
     m, r, w = a.shape
     return a.reshape(m, r, w // LANES, LANES).transpose(0, 2, 1, 3).reshape(-1, LANES)
@@ -239,8 +292,10 @@
             a = a.reshape(mats, wide // LANES, rows, LANES).transpose(0, 2, 1, 3)
             return a.reshape(mats, rows, wide)
 
-        new_w, new_m = make_kernel(fs, tp, mats, wide)(
-            flat(slopes_in), flat(moments_in), flat(weights_in)
+        new_w, new_m = store(
+            *make_kernel(fs, tp, mats, wide)(
+                flat(slopes_in), flat(moments_in), flat(weights_in)
+            )
         )
         return unflat(new_w), unflat(new_m)
 

time: 123 us -> 105 us (0.85)
  Pallas kernels: 114 us -> 105 us
  local copies, waits for them, and re-layouts: 7.41 us -> 0 us
    pallas_call x1, Pallas kernels: 114 us -> 103 us  [body(): make_kernel(fs, tp, mats, wide)]
    unnamed x8 -> x0, local copies, waits for them, and re-layouts: 7.41 us -> none
    pallas_call x0 -> x1, Pallas kernels: none -> 2.03 us  [store(): pl.pallas_call(kernel, out_shape=[jax.ShapeDtypeStruct(new_w.shape, new_w...]
where the time goes in v2:
time: 105 us
  Pallas kernels  105 us (100%)
    pallas_call x1, Pallas kernels, body(): make_kernel(fs, tp, mats, wide)  103 us

profile of v2, /device:TPU:1, one launch (start us, length us, event | category | flops | bytes accessed | tf_op | source)
XLA Modules:
  0.0 105.2 jit_solution(16113917461247871390)
XLA Ops:
  0.6 102.6 %step.1 = (f32[4096,128]{1,0:T(8,128)S(1)}, f32[4096,128]{1,0:T(8,128)S(1)}) custom-call(f32[4096,128]{1,0:T(8,128)} %bitcast.25, f32[4096,128]{1,0:T(8,128)} %bitcast.26, f32[4096,128]{1,0:T(8,128)} %bitcast.27), custom_call_target="tpu_custom_call" | custom-call | tf_op jit(solution)/shard_map/step/pallas_call | solution.py:296
  103.2 2.0 %store.1 = (f32[4096,128]{1,0:T(8,128)}, f32[4096,128]{1,0:T(8,128)}) custom-call(f32[4096,128]{1,0:T(8,128)S(1)} %get-tuple-element.6.w_in, f32[4096,128]{1,0:T(8,128)S(1)} %get-tuple-element.7.m_in), custom_call_target="tpu_custom_call" | custom-call | tf_op jit(solution)/shard_map/store/pallas_call | solution.py:269

commit v3 on v2

--- a/solution.py
+++ b/solution.py
@@ -11,7 +11,7 @@
 LANES = 128
 SIDE = 128
 RING = 8
-AROUND = (0, 1, 7, 2, 6, 3, 5, 4)
+AROUND = (4, 3, 5, 2, 6, 1, 7, 0)
 MESH = pl.DeviceIdType.MESH
 
 
@@ -72,16 +72,17 @@
 
         def peers(fars, visit):
             def at(n, carry):
+                n = 8 - n
                 near = (x + n // 2) % 4 * 2 + (c + n % 2) % 2
                 for far in fars:
                     visit(rings[far] + near)
                 return carry
 
             if 0 in fars:
+                lax.fori_loop(1, 8, at, 0)
                 for far in fars:
                     if far:
                         visit(rings[far] + x * 2 + c)
-                lax.fori_loop(1, 8, at, 0)
             else:
                 lax.fori_loop(0, 8, at, 0)
 
@@ -230,7 +231,8 @@
 
     total = chunks * part
     buf = pltpu.VMEM((total, LANES), jnp.float32)
-    scratch = [buf] * 6 + [
+    strided = pltpu.VMEM((total + span, LANES), jnp.float32)
+    scratch = [buf] * 2 + [strided] * 2 + [buf] * 2 + [
         pltpu.VMEM((SIDE, wide), jnp.float32),
         pltpu.VMEM((SIDE, wide), jnp.float32),
         pltpu.VMEM((2, chunks, tp, SIDE, SIDE), jnp.float32),

time: 105 us -> 105 us (level)
  no operation moved by 1% of the time
where the time goes in v3:
time: 105 us
  Pallas kernels  104 us (99%)
    pallas_call x1, Pallas kernels, body(): make_kernel(fs, tp, mats, wide)  102 us

profile of v3, /device:TPU:1, one launch (start us, length us, event | category | flops | bytes accessed | tf_op | source)
XLA Modules:
  0.0 104.7 jit_solution(18111722803184660767)
XLA Ops:
  0.6 102.0 %step.1 = (f32[4096,128]{1,0:T(8,128)S(1)}, f32[4096,128]{1,0:T(8,128)S(1)}) custom-call(f32[4096,128]{1,0:T(8,128)} %bitcast.25, f32[4096,128]{1,0:T(8,128)} %bitcast.26, f32[4096,128]{1,0:T(8,128)} %bitcast.27), custom_call_target="tpu_custom_call" | custom-call | tf_op jit(solution)/shard_map/step/pallas_call | solution.py:298
  102.6 2.0 %store.1 = (f32[4096,128]{1,0:T(8,128)}, f32[4096,128]{1,0:T(8,128)}) custom-call(f32[4096,128]{1,0:T(8,128)S(1)} %get-tuple-element.6.w_in, f32[4096,128]{1,0:T(8,128)S(1)} %get-tuple-element.7.m_in), custom_call_target="tpu_custom_call" | custom-call | tf_op jit(solution)/shard_map/store/pallas_call | solution.py:271

commit v4 on v3

--- a/solution.py
+++ b/solution.py
@@ -108,6 +108,28 @@
                 ).start()
 
             peers(fars, send)
+
+        def send_last(k, zs):
+            def at(n, carry):
+                n = 8 - n
+                near = (x + n // 2) % 4 * 2 + (c + n % 2) % 2
+                for to in zs:
+                    j = to * 8 + near
+
+                    @pl.when(j != me)
+                    def _():
+                        pltpu.make_async_remote_copy(
+                            src_ref=res.at[block(k, j)],
+                            dst_ref=back.at[block(k, me)],
+                            send_sem=b_send,
+                            recv_sem=b_recv.at[k],
+                            device_id=(j, col),
+                            device_id_type=MESH,
+                        ).start()
+
+                return carry
+
+            lax.fori_loop(1, 9, at, 0)
 
         def wait_rows(buf, n, sem):
             rows = pl.ds(0, n * span)
@@ -212,7 +234,15 @@
                 out = dot(mixed, x3_buf[:, LANES * t : LANES * (t + 1)])
                 for r in range(2):
                     res[pl.ds(k * part + 2 * t + r, fs, stride=span), :] = out[fs * r : fs * (r + 1)]
-            send_all(res, back, k, b_send, b_recv)
+            @pl.when(k + 1 < chunks)
+            def _():
+                send_all(res, back, k, b_send, b_recv)
+
+            @pl.when(k + 1 == chunks)
+            def _():
+                send_last(k, (0, 1))
+                send_last(k, (2, 3, 7, 4, 6, 5))
+
             back[block(k, me), :] = res[block(k, me), :]
             return carry
 

time: 105 us -> 104 us (level)
    pallas_call x1, Pallas kernels: 102 us -> 101 us  [body(): make_kernel(fs, tp, mats, wide)]
where the time goes in v4:
time: 104 us
  Pallas kernels  103 us (99%)
    pallas_call x1, Pallas kernels, body(): make_kernel(fs, tp, mats, wide)  101 us

profile of v4, /device:TPU:1, one launch (start us, length us, event | category | flops | bytes accessed | tf_op | source)
XLA Modules:
  0.0 103.6 jit_solution(5538958635583179956)
XLA Ops:
  0.6 100.9 %step.1 = (f32[4096,128]{1,0:T(8,128)S(1)}, f32[4096,128]{1,0:T(8,128)S(1)}) custom-call(f32[4096,128]{1,0:T(8,128)} %bitcast.25, f32[4096,128]{1,0:T(8,128)} %bitcast.26, f32[4096,128]{1,0:T(8,128)} %bitcast.27), custom_call_target="tpu_custom_call" | custom-call | tf_op jit(solution)/shard_map/step/pallas_call | solution.py:328
  101.6 2.0 %store.1 = (f32[4096,128]{1,0:T(8,128)}, f32[4096,128]{1,0:T(8,128)}) custom-call(f32[4096,128]{1,0:T(8,128)S(1)} %get-tuple-element.6.w_in, f32[4096,128]{1,0:T(8,128)S(1)} %get-tuple-element.7.m_in), custom_call_target="tpu_custom_call" | custom-call | tf_op jit(solution)/shard_map/store/pallas_call | solution.py:301

commit v5 on v4

--- a/solution.py
+++ b/solution.py
@@ -240,8 +240,8 @@
 
             @pl.when(k + 1 == chunks)
             def _():
-                send_last(k, (0, 1))
-                send_last(k, (2, 3, 7, 4, 6, 5))
+                send_last(k, (2, 0, 1))
+                send_last(k, (3, 7, 4, 6, 5))
 
             back[block(k, me), :] = res[block(k, me), :]
             return carry

time: 104 us -> 105 us (level)
  Pallas kernels: 103 us -> 105 us
    pallas_call x1, Pallas kernels: 101 us -> 103 us  [body(): make_kernel(fs, tp, mats, wide)]
where the time goes in v5:
time: 105 us
  Pallas kernels  105 us (100%)
    pallas_call x1, Pallas kernels, body(): make_kernel(fs, tp, mats, wide)  103 us

profile of v5, /device:TPU:1, one launch (start us, length us, event | category | flops | bytes accessed | tf_op | source)
XLA Modules:
  0.0 105.3 jit_solution(16390487384200604329)
XLA Ops:
  0.6 102.6 %step.1 = (f32[4096,128]{1,0:T(8,128)S(1)}, f32[4096,128]{1,0:T(8,128)S(1)}) custom-call(f32[4096,128]{1,0:T(8,128)} %bitcast.25, f32[4096,128]{1,0:T(8,128)} %bitcast.26, f32[4096,128]{1,0:T(8,128)} %bitcast.27), custom_call_target="tpu_custom_call" | custom-call | tf_op jit(solution)/shard_map/step/pallas_call | solution.py:328
  103.3 2.0 %store.1 = (f32[4096,128]{1,0:T(8,128)}, f32[4096,128]{1,0:T(8,128)}) custom-call(f32[4096,128]{1,0:T(8,128)S(1)} %get-tuple-element.6.w_in, f32[4096,128]{1,0:T(8,128)S(1)} %get-tuple-element.7.m_in), custom_call_target="tpu_custom_call" | custom-call | tf_op jit(solution)/shard_map/store/pallas_call | solution.py:301
